TPU v7x, 32 devices: a whole 2x2x4 slice. The times are simulated.
32 devices in a mesh: dp: 8 (over y, x, core), mp: 4 (over z).
Axes of the slice: x: 2, y: 2, z: 4, core: 2. Of those that a mesh axis runs over, the one named last changes fastest.
Arguments:
- hidden_in: bfloat16 [4096, 2048], P('dp'), may hold values from -6 to 6
- cotangent: bfloat16 [4096, 2048], P('dp'), may hold values from -6 to 6
- segments: int32 [8, 512], P('dp'), may hold values from 0 to 5, never falling along the last dimension, each value on 1 to 256 neighbouring positions
- live_counts: int32 [8], P('dp'), may hold values from 128 to 512, as said below
- w_query: bfloat16 [2048, 2048], P('dp', 'mp'), may hold values from -0.125 to 0.125
- w_key: bfloat16 [2048, 2048], P('dp', 'mp'), may hold values from -0.125 to 0.125
- w_value: bfloat16 [2048, 2048], P('dp', 'mp'), may hold values from -0.125 to 0.125
- w_output: bfloat16 [2048, 2048], P('mp', 'dp'), may hold values from -0.125 to 0.125
- w_gate: bfloat16 [2048, 8192], P('dp', 'mp'), may hold values from -0.125 to 0.125
- w_up: bfloat16 [2048, 8192], P('dp', 'mp'), may hold values from -0.125 to 0.125
- w_down: bfloat16 [8192, 2048], P('mp', 'dp'), may hold values from -0.0625 to 0.0625
- query_gain: float32 [2048], P('mp'), may hold values from 0.5 to 1.5
- key_gain: float32 [2048], P('mp'), may hold values from 0.5 to 1.5
- attn_gain: float32 [2048], replicated, may hold values from 0.5 to 1.5
- ffn_gain: float32 [2048], replicated, may hold values from 0.5 to 1.5
Outputs:
- hidden_out: bfloat16 [4096, 2048], P('dp')
- grad_in: float32 [4096, 2048], P('dp')
- grad_query: float32 [2048, 2048], P('dp', 'mp')
- grad_key: float32 [2048, 2048], P('dp', 'mp')
- grad_value: float32 [2048, 2048], P('dp', 'mp')
- grad_output_w: float32 [2048, 2048], P('mp', 'dp')
- grad_gate: float32 [2048, 8192], P('dp', 'mp')
- grad_up: float32 [2048, 8192], P('dp', 'mp')
- grad_down: float32 [8192, 2048], P('mp', 'dp')
- grad_query_gain: float32 [2048], P('mp')
- grad_key_gain: float32 [2048], P('mp')
- grad_attn_gain: float32 [2048], replicated
- grad_ffn_gain: float32 [2048], replicated
Inputs may be any that keep to these rules, and one draw needn't show every extreme that they name: Within the rows of one index of dp, segments never fall; each of the 6 documents has 1 to 256 rows and one has exactly 256. `live_counts`: rows of a block at or after its live count are padding; some index of dp has 512 live rows and some has 128.
All inputs are finite; a program needn't handle non-finite values.
Results may differ from a plain program's by a relative error of at most 0.017.
Values may be sent and summed in bfloat16 or wider, within the bound.
A program may use at most 256 MiB of HBM per device.

v0:
```python
import math
import jax
import jax.numpy as jnp
from jax import lax
from jax.sharding import PartitionSpec as P

HD = 128
EPS = 1e-06
THETA = 500000.0


def doc_positions(seg_row):
    row_count = seg_row.shape[0]
    row_index = jnp.arange(row_count, dtype=jnp.int32)
    change = jnp.concatenate([jnp.ones((1,), dtype=bool), seg_row[1:] != seg_row[:-1]])
    doc_start = lax.cummax(jnp.where(change, row_index, jnp.zeros_like(row_index)), axis=0)
    return (row_index - doc_start).astype(jnp.float32)


def rotary_tables(positions, head_size):
    half_size = head_size // 2
    inv_freq = THETA ** (-(jnp.arange(half_size, dtype=jnp.float32) * (2.0 / head_size)))
    angles = positions[:, None] * inv_freq[None, :]
    return (jnp.cos(angles)[:, None, :], jnp.sin(angles)[:, None, :])


def rotate(values, cos_tab, sin_tab):
    half_size = values.shape[2] // 2
    first_half = values[:, :, :half_size]
    second_half = values[:, :, half_size:]
    return jnp.concatenate(
        [
            first_half * cos_tab - second_half * sin_tab,
            second_half * cos_tab + first_half * sin_tab,
        ],
        axis=2,
    )


def rotate_back(grads, cos_tab, sin_tab):
    half_size = grads.shape[2] // 2
    first_half = grads[:, :, :half_size]
    second_half = grads[:, :, half_size:]
    return jnp.concatenate(
        [
            first_half * cos_tab + second_half * sin_tab,
            second_half * cos_tab - first_half * sin_tab,
        ],
        axis=2,
    )


def block_mask(seg_row, offset, block_rows):
    row_index = jnp.arange(seg_row.shape[0])
    same = seg_row[offset : offset + block_rows, None] == seg_row[None, :]
    return same & (row_index[:, None] >= row_index[None, :])


def block_scores(q_blk, k_bf, allowed, score_scale):
    scores = (
        jnp.einsum("qhe,khe->hqk", q_blk, k_bf, preferred_element_type=jnp.float32) * score_scale
    )
    return jnp.where(allowed[None], scores, jnp.float32(-1e30))


def attend_forward(q_bf, k_bf, v_bf, seg_row, score_scale):
    row_count = q_bf.shape[0]
    block_rows = min(512, row_count)
    allowed = block_mask(seg_row, 0, block_rows)
    scores = block_scores(q_bf, k_bf, allowed, score_scale)
    row_max = jnp.max(scores, axis=2, keepdims=True)
    lse = row_max + jnp.log(jnp.sum(jnp.exp(scores - row_max), axis=2, keepdims=True))
    probs = jnp.exp(scores - lse).astype(jnp.bfloat16)
    outputs = jnp.einsum("hqk,khe->qhe", probs, v_bf, preferred_element_type=jnp.float32)
    lse_parts = [lse]
    return (outputs.astype(jnp.bfloat16), lse_parts)


def attend_backward(q_bf, k_bf, v_bf, o_bf, do_bf, lse_parts, seg_row, score_scale):
    row_count = q_bf.shape[0]
    block_rows = min(512, row_count)
    dq_parts = []
    dk_acc = jnp.zeros(k_bf.shape, jnp.float32)
    dv_acc = jnp.zeros(v_bf.shape, jnp.float32)
    for part_index, offset in enumerate(range(0, row_count, block_rows)):
        allowed = block_mask(seg_row, offset, block_rows)
        scores = block_scores(q_bf, k_bf, allowed, score_scale)
        probs = jnp.exp(scores - lse_parts[part_index])
        probs_bf = probs.astype(jnp.bfloat16)
        dprob = jnp.einsum("qhe,khe->hqk", do_bf, v_bf, preferred_element_type=jnp.float32)
        delta = jnp.transpose(
            jnp.sum(do_bf.astype(jnp.float32) * o_bf.astype(jnp.float32), axis=2)
        )[:, :, None]
        dscore = (probs * (dprob - delta)).astype(jnp.bfloat16)
        dq_parts.append(
            jnp.einsum("hqk,khe->qhe", dscore, k_bf, preferred_element_type=jnp.float32)
            * score_scale
        )
        dk_acc = (
            jnp.einsum("hqk,qhe->khe", dscore, q_bf, preferred_element_type=jnp.float32)
            * score_scale
        )
        dv_acc = jnp.einsum("hqk,qhe->khe", probs_bf, do_bf, preferred_element_type=jnp.float32)
    return (dq_parts[0], dk_acc, dv_acc.astype(jnp.bfloat16))


def norm_back(raw, inv_scale, gained, row_sums, width):
    return inv_scale * gained - raw * inv_scale**3 * (row_sums[:, None] / width)


def on_device(
    hidden_in,
    cotangent,
    segments,
    live_counts,
    w_query,
    w_key,
    w_value,
    w_output,
    w_gate,
    w_up,
    w_down,
    query_gain,
    key_gain,
    attn_gain,
    ffn_gain,
):
    gathered = (
        lax.all_gather(w_query, "dp", axis=0, tiled=True),
        lax.all_gather(w_key, "dp", axis=0, tiled=True),
        lax.all_gather(w_value, "dp", axis=0, tiled=True),
        lax.all_gather(w_output, "dp", axis=1, tiled=True),
        lax.all_gather(w_gate, "dp", axis=0, tiled=True),
        lax.all_gather(w_up, "dp", axis=0, tiled=True),
        lax.all_gather(w_down, "dp", axis=1, tiled=True),
    )
    wq_full, wk_full, wv_full, wo_full, wg_full, wu_full, wd_full = gathered
    seg_row = segments[0]
    live_n = live_counts[0]
    row_count, width = hidden_in.shape
    local_width = wq_full.shape[1]
    heads_here = local_width // HD
    score_scale = 1.0 / math.sqrt(HD)
    live_mask = (jnp.arange(row_count, dtype=jnp.int32) < live_n).astype(jnp.float32)[:, None]
    cos_tab, sin_tab = rotary_tables(doc_positions(seg_row), HD)
    q_proj = jnp.dot(hidden_in, wq_full, preferred_element_type=jnp.float32)
    k_proj = jnp.dot(hidden_in, wk_full, preferred_element_type=jnp.float32)
    v_bf = jnp.dot(hidden_in, wv_full, preferred_element_type=jnp.float32).astype(jnp.bfloat16)
    sq_query, sq_key = lax.psum(
        (jnp.sum(q_proj * q_proj, axis=1), jnp.sum(k_proj * k_proj, axis=1)), "mp"
    )
    inv_q = lax.rsqrt(sq_query[:, None] / width + EPS)
    inv_k = lax.rsqrt(sq_key[:, None] / width + EPS)
    q_rot = rotate(
        (q_proj * inv_q * query_gain).reshape(row_count, heads_here, HD), cos_tab, sin_tab
    ).astype(jnp.bfloat16)
    k_rot = rotate(
        (k_proj * inv_k * key_gain).reshape(row_count, heads_here, HD), cos_tab, sin_tab
    ).astype(jnp.bfloat16)
    v_heads = v_bf.reshape(row_count, heads_here, HD)
    o_bf, lse_parts = attend_forward(q_rot, k_rot, v_heads, seg_row, score_scale)
    o_flat = o_bf.reshape(row_count, local_width)
    attn_raw = lax.psum(jnp.dot(o_flat, wo_full, preferred_element_type=jnp.float32), "mp")
    inv_a = lax.rsqrt(jnp.mean(attn_raw * attn_raw, axis=1, keepdims=True) + EPS)
    h_mid = hidden_in.astype(jnp.float32) + attn_raw * inv_a * attn_gain
    h_bf = h_mid.astype(jnp.bfloat16)
    gate_pre = jnp.dot(h_bf, wg_full, preferred_element_type=jnp.float32)
    up_pre = jnp.dot(h_bf, wu_full, preferred_element_type=jnp.float32)
    act_bf = (jax.nn.silu(gate_pre) * up_pre).astype(jnp.bfloat16)
    ffn_raw = lax.psum(jnp.dot(act_bf, wd_full, preferred_element_type=jnp.float32), "mp")
    inv_f = lax.rsqrt(jnp.mean(ffn_raw * ffn_raw, axis=1, keepdims=True) + EPS)
    hidden_out = (live_mask * (h_mid + ffn_raw * inv_f * ffn_gain)).astype(jnp.bfloat16)
    back_weights = (
        lax.all_gather(w_query, "dp", axis=0, tiled=True),
        lax.all_gather(w_key, "dp", axis=0, tiled=True),
        lax.all_gather(w_value, "dp", axis=0, tiled=True),
        lax.all_gather(w_output, "dp", axis=1, tiled=True),
        lax.all_gather(w_gate, "dp", axis=0, tiled=True),
        lax.all_gather(w_up, "dp", axis=0, tiled=True),
        lax.all_gather(w_down, "dp", axis=1, tiled=True),
    )
    wq_back, wk_back, wv_back, wo_back, wg_back, wu_back, wd_back = back_weights
    dy = live_mask * cotangent.astype(jnp.float32)
    g_ffn_gain = jnp.sum(dy * ffn_raw * inv_f, axis=0)
    gained_f = ffn_gain * dy
    d_ffn = norm_back(ffn_raw, inv_f, gained_f, jnp.sum(gained_f * ffn_raw, axis=1), width).astype(
        jnp.bfloat16
    )
    d_act = jnp.dot(d_ffn, wd_back.T, preferred_element_type=jnp.float32)
    sig = jax.nn.sigmoid(gate_pre)
    d_up = (d_act * gate_pre * sig).astype(jnp.bfloat16)
    d_gate = (d_act * up_pre * sig * (1.0 + gate_pre * (1.0 - sig))).astype(jnp.bfloat16)
    ffn_part = jnp.dot(d_gate, wg_back.T, preferred_element_type=jnp.float32) + jnp.dot(
        d_up, wu_back.T, preferred_element_type=jnp.float32
    )
    dh = dy + lax.psum(ffn_part, "mp")
    g_down = jnp.dot(act_bf.T, d_ffn, preferred_element_type=jnp.float32)
    g_gate = jnp.dot(h_bf.T, d_gate, preferred_element_type=jnp.float32)
    g_up = jnp.dot(h_bf.T, d_up, preferred_element_type=jnp.float32)
    g_attn_gain = jnp.sum(dh * attn_raw * inv_a, axis=0)
    gained_a = attn_gain * dh
    d_attn = norm_back(
        attn_raw, inv_a, gained_a, jnp.sum(gained_a * attn_raw, axis=1), width
    ).astype(jnp.bfloat16)
    d_heads = jnp.dot(d_attn, wo_back.T, preferred_element_type=jnp.float32).astype(jnp.bfloat16)
    g_output = jnp.dot(o_flat.T, d_attn, preferred_element_type=jnp.float32)
    dq_rot, dk_rot, d_val = attend_backward(
        q_rot,
        k_rot,
        v_heads,
        o_bf,
        d_heads.reshape(row_count, heads_here, HD),
        lse_parts,
        seg_row,
        score_scale,
    )
    dq_norm = rotate_back(dq_rot, cos_tab, sin_tab).reshape(row_count, local_width)
    dk_norm = rotate_back(dk_rot, cos_tab, sin_tab).reshape(row_count, local_width)
    g_query_gain = jnp.sum(dq_norm * q_proj * inv_q, axis=0)
    g_key_gain = jnp.sum(dk_norm * k_proj * inv_k, axis=0)
    gained_q = query_gain * dq_norm
    gained_k = key_gain * dk_norm
    sums_query, sums_key = lax.psum(
        (jnp.sum(gained_q * q_proj, axis=1), jnp.sum(gained_k * k_proj, axis=1)), "mp"
    )
    dq_bf = norm_back(q_proj, inv_q, gained_q, sums_query, width).astype(jnp.bfloat16)
    dk_bf = norm_back(k_proj, inv_k, gained_k, sums_key, width).astype(jnp.bfloat16)
    dv_bf = d_val.reshape(row_count, local_width)
    input_part = (
        jnp.dot(dq_bf, wq_back.T, preferred_element_type=jnp.float32)
        + jnp.dot(dk_bf, wk_back.T, preferred_element_type=jnp.float32)
        + jnp.dot(dv_bf, wv_back.T, preferred_element_type=jnp.float32)
    )
    grad_in = dh + lax.psum(input_part.astype(jnp.bfloat16), "mp").astype(jnp.float32)
    g_query = jnp.dot(hidden_in.T, dq_bf, preferred_element_type=jnp.float32)
    g_key = jnp.dot(hidden_in.T, dk_bf, preferred_element_type=jnp.float32)
    g_value = jnp.dot(hidden_in.T, dv_bf, preferred_element_type=jnp.float32)
    owned = (
        lax.psum_scatter(g_query, "dp", scatter_dimension=0, tiled=True),
        lax.psum_scatter(g_key, "dp", scatter_dimension=0, tiled=True),
        lax.psum_scatter(g_value, "dp", scatter_dimension=0, tiled=True),
        lax.psum_scatter(g_output, "dp", scatter_dimension=1, tiled=True),
        lax.psum_scatter(g_gate, "dp", scatter_dimension=0, tiled=True),
        lax.psum_scatter(g_up, "dp", scatter_dimension=0, tiled=True),
        lax.psum_scatter(g_down, "dp", scatter_dimension=1, tiled=True),
    )
    gain_totals = lax.psum((g_query_gain, g_key_gain, g_attn_gain, g_ffn_gain), "dp")
    return (
        hidden_out,
        grad_in,
        owned[0],
        owned[1],
        owned[2],
        owned[3],
        owned[4],
        owned[5],
        owned[6],
        gain_totals[0],
        gain_totals[1],
        gain_totals[2],
        gain_totals[3],
    )


def solution(mesh):
    return jax.shard_map(
        on_device,
        mesh=mesh,
        in_specs=(
            P("dp", None),
            P("dp", None),
            P("dp", None),
            P("dp"),
            P("dp", "mp"),
            P("dp", "mp"),
            P("dp", "mp"),
            P("mp", "dp"),
            P("dp", "mp"),
            P("dp", "mp"),
            P("mp", "dp"),
            P("mp"),
            P("mp"),
            P(),
            P(),
        ),
        out_specs=(
            P("dp", None),
            P("dp", None),
            P("dp", "mp"),
            P("dp", "mp"),
            P("dp", "mp"),
            P("mp", "dp"),
            P("dp", "mp"),
            P("dp", "mp"),
            P("mp", "dp"),
            P("mp"),
            P("mp"),
            P(),
            P(),
        ),
        check_vma=False,
    )
```

profile of v0, /device:TPU:0, one launch (start us, length us, event | category | flops | bytes accessed | tf_op | source)
XLA Modules:
  0.0 1542.0 jit_solution(11089845251164984126)
XLA Ops:
  12.5 1.8 multiply_cosine_fusion
  14.4 26.0 %all-gather.12.cloned.1.call-done = bf16[2048,512]{1,0:T(8,128)(2,1)} async-done(((bf16[256,512]{1,0:T(8,128)(2,1)}), bf16[2048,512]{1,0:T(8,128)(2,1)}) %all-gather.12.cloned.1.call-update) | async-done | bytes 2097168 | tf_op jit(solution)/shard_map/all_gather | solution.py:130
  40.4 3.5 multiply_reduce_fusion.9
  44.0 26.1 %all-gather.10.cloned.1.call-done = bf16[2048,512]{1,0:T(8,128)(2,1)} async-done(((bf16[256,512]{1,0:T(8,128)(2,1)}), bf16[2048,512]{1,0:T(8,128)(2,1)}) %all-gather.10.cloned.1.call-update) | async-done | bytes 2097168 | tf_op jit(solution)/shard_map/all_gather | solution.py:129
  70.1 3.9 multiply_reduce_fusion.10
  74.0 11.8 all-reduce.2
  87.0 2.4 copy.82
  89.3 2.4 copy.81
  94.1 2.4 copy.80
  96.5 2.4 copy.79
  98.8 2.9 subtract_convert_fusion.5
  103.2 2.0 copy-done.7
  106.2 3.0 convolution_convert_fusion.1
  110.0 2.2 convolution_convert_fusion.3
  112.2 17.5 %all-gather.14.cloned.1.call-done = bf16[512,2048]{1,0:T(8,128)(2,1)} async-done(((bf16[512,256]{1,0:T(8,128)(2,1)}), bf16[512,2048]{1,0:T(8,128)(2,1)}) %all-gather.14.cloned.1.call-update) | async-done | bytes 2097168 | tf_op jit(solution)/shard_map/all_gather | solution.py:132
  129.7 5.0 fusion.24
  137.1 152.8 %all-reduce.8.cloned.1.call-done = f32[512,2048]{1,0:T(8,128)} async-done(((f32[512,2048]{1,0:T(8,128)}), f32[512,2048]{1,0:T(8,128)}) %all-reduce.8.cloned.1.call-update) | async-done | bytes 4194320 | tf_op jit(solution)/shard_map/psum | solution.py:163
  289.9 2.7 multiply_reduce_fusion.5
  293.3 2.1 fusion.4
  295.4 49.5 %all-gather.16.cloned.1.call-done = bf16[2048,2048]{1,0:T(8,128)(2,1)} async-done(((bf16[256,2048]{1,0:T(8,128)(2,1)}), bf16[2048,2048]{1,0:T(8,128)(2,1)}) %all-gather.16.cloned.1.call-update) | async-done | bytes 8388624 | tf_op jit(solution)/shard_map/all_gather | solution.py:133
  344.9 10.6 fusion.25
  355.4 45.6 %all-gather.18.cloned.1.call-done = bf16[2048,2048]{1,0:T(8,128)(2,1)} async-done(((bf16[256,2048]{1,0:T(8,128)(2,1)}), bf16[2048,2048]{1,0:T(8,128)(2,1)}) %all-gather.18.cloned.1.call-update) | async-done | bytes 8388624 | tf_op jit(solution)/shard_map/all_gather | solution.py:134
  401.0 12.5 multiply_convert_fusion.4
  413.5 45.3 %all-gather.20.cloned.1.call-done = bf16[2048,2048]{1,0:T(8,128)(2,1)} async-done(((bf16[2048,256]{1,0:T(8,128)(2,1)}), bf16[2048,2048]{1,0:T(8,128)(2,1)}) %all-gather.20.cloned.1.call-update) | async-done | bytes 8388624 | tf_op jit(solution)/shard_map/all_gather | solution.py:135
  458.8 10.5 fusion.26
  470.4 154.0 %all-reduce.10.cloned.1.call-done = f32[512,2048]{1,0:T(8,128)} async-done(((f32[512,2048]{1,0:T(8,128)}), f32[512,2048]{1,0:T(8,128)}) %all-reduce.10.cloned.1.call-update) | async-done | bytes 4194320 | tf_op jit(solution)/shard_map/psum | solution.py:170
  624.4 2.7 multiply_reduce_fusion.4
  627.9 3.0 multiply_reduce_fusion
  630.8 14.1 multiply_convert_fusion.1
  644.9 7.8 fusion.27
  652.7 9.6 convolution_add_fusion
  662.5 153.9 %all-reduce.12.cloned.1.call-done = f32[512,2048]{1,0:T(8,128)} async-done(((f32[512,2048]{1,0:T(8,128)}), f32[512,2048]{1,0:T(8,128)}) %all-reduce.12.cloned.1.call-update) | async-done | bytes 4194320 | tf_op jit(solution)/shard_map/psum | solution.py:196
  816.4 5.0 multiply_reduce_fusion.1
  823.5 5.5 subtract_convert_fusion
  832.0 2.2 convolution_convert_fusion.2
  838.1 2.0 multiply_add_fusion.1
  841.5 2.6 copy.63
  845.6 2.9 pad_maximum_fusion
  848.6 2.5 copy.59
  851.1 1.9 fusion.10
  852.9 9.6 all-reduce.1
  862.6 1.9 subtract_convert_fusion.3
  864.5 1.6 subtract_convert_fusion.2
  869.6 2.7 add_convert_fusion
  872.4 3.2 convolution_bitcast_fusion
  875.8 3.2 convolution_bitcast_fusion.2
  879.1 3.2 convolution_bitcast_fusion.1
  882.4 5.0 fusion.30
  887.7 13.6 fusion.20
  901.4 12.5 fusion.32
  914.2 12.5 fusion.31
  926.8 24.9 %all-reduce = (f32[512]{0:T(512)}, f32[512]{0:T(512)}, f32[2048]{0:T(1024)}, f32[2048]{0:T(1024)}) all-reduce(f32[512]{0:T(512)S(1)} %get-tuple-element.45, f32[512]{0:T(512)S(1)} %get-tuple-element.43, f32[2048]{0:T(1024)S(1)} %get-tuple-element.39, f32[2048]{0:T(1024)S(1)} %get-tuple-element.41), channel_id=1, replica_groups=mesh['dp'=8,'mp'=4] {'dp'}, use_global_device_ids=true, to_apply=%region_29.30 | all-reduce | flops 5120 | bytes 40960 | tf_op jit(solution)/shard_map/psum | solution.py:247
  951.6 5.6 all-reduce.14.cloned.1.call-done
  957.2 6.1 convert_add_fusion
  963.3 47.3 %reduce-scatter.12.cloned.1.call-done = f32[256,512]{0,1:T(8,128)} async-done(((f32[2048,512]{0,1:T(8,128)}), f32[256,512]{0,1:T(8,128)}) %reduce-scatter.12.cloned.1.call-update) | async-done | bytes 524304 | tf_op jit(solution)/shard_map/reduce_scatter | solution.py:241
  1010.5 2.0 copy.67
  1012.6 52.4 %reduce-scatter.8.cloned.1.call-done = f32[256,512]{0,1:T(8,128)} async-done(((f32[2048,512]{0,1:T(8,128)}), f32[256,512]{0,1:T(8,128)}) %reduce-scatter.8.cloned.1.call-update) | async-done | bytes 524304 | tf_op jit(solution)/shard_map/reduce_scatter | solution.py:239
  1065.0 2.0 copy.65
  1067.1 52.3 %reduce-scatter.10.cloned.1.call-done = f32[256,512]{0,1:T(8,128)} async-done(((f32[2048,512]{0,1:T(8,128)}), f32[256,512]{0,1:T(8,128)}) %reduce-scatter.10.cloned.1.call-update) | async-done | bytes 524304 | tf_op jit(solution)/shard_map/reduce_scatter | solution.py:240
  1119.4 2.0 copy.66
  1121.4 52.9 %reduce-scatter.14.cloned.1.call-done = f32[512,256]{1,0:T(8,128)} async-done(((f32[512,2048]{1,0:T(8,128)}), f32[512,256]{1,0:T(8,128)}) %reduce-scatter.14.cloned.1.call-update) | async-done | bytes 524304 | tf_op jit(solution)/shard_map/reduce_scatter | solution.py:242
  1174.2 120.0 %reduce-scatter.20.cloned.1.call-done = f32[2048,256]{1,0:T(8,128)} async-done(((f32[2048,2048]{1,0:T(8,128)}), f32[2048,256]{1,0:T(8,128)}) %reduce-scatter.20.cloned.1.call-update) | async-done | bytes 2097168 | tf_op jit(solution)/shard_map/reduce_scatter | solution.py:245
  1294.3 120.2 %reduce-scatter.18.cloned.1.call-done = f32[256,2048]{1,0:T(8,128)} async-done(((f32[2048,2048]{1,0:T(8,128)}), f32[256,2048]{1,0:T(8,128)}) %reduce-scatter.18.cloned.1.call-update) | async-done | bytes 2097168 | tf_op jit(solution)/shard_map/reduce_scatter | solution.py:244
  1414.5 120.2 %reduce-scatter.16.cloned.1.call-done = f32[256,2048]{1,0:T(8,128)} async-done(((f32[2048,2048]{1,0:T(8,128)}), f32[256,2048]{1,0:T(8,128)}) %reduce-scatter.16.cloned.1.call-update) | async-done | bytes 2097168 | tf_op jit(solution)/shard_map/reduce_scatter | solution.py:243
  (146 shorter events, 32.8 us)
Async XLA Ops:
  7.2 33.2 %all-gather.12.cloned.1.call-start = ((), (), s32[]{:S(2)}) async-start(), calls=%async_computation.9 | async-start | bytes 2359296 | tf_op jit(solution)/shard_map/all_gather | solution.py:130
  7.9 62.2 %all-gather.10.cloned.1.call-start = ((), (), s32[]{:S(2)}) async-start(), calls=%async_computation.8 | async-start | bytes 2359296 | tf_op jit(solution)/shard_map/all_gather | solution.py:129
  8.7 97.5 %all-gather.8.cloned.1.call-start = ((), (), s32[]{:S(2)}) async-start(), calls=%async_computation.7 | async-start | bytes 2359296 | tf_op jit(solution)/shard_map/all_gather | solution.py:131
  9.4 120.3 %all-gather.14.cloned.1.call-start = ((), (), s32[]{:S(2)}) async-start(), calls=%async_computation.10 | async-start | bytes 2359296 | tf_op jit(solution)/shard_map/all_gather | solution.py:132
  10.0 279.9 %all-reduce.8.cloned.1.call-start = ((), (), s32[]{:S(2)}) async-start(), calls=%async_computation.11 | async-start | bytes 8388608 | tf_op jit(solution)/shard_map/psum | solution.py:163
  14.4 55.7 %copy-start.2 = (bf16[512,2048]{1,0:T(8,128)(2,1)S(1)}, bf16[512,2048]{1,0:T(8,128)(2,1)}, u32[]{:S(2)}) copy-start(bf16[512,2048]{1,0:T(8,128)(2,1)} %param.15) | copy-start | bytes 6291460
  43.9 41.8 %copy-start.35 = (f32[512]{0:T(512)S(1)}, f32[512]{0:T(512)}, u32[]{:S(2)}) copy-start(f32[512]{0:T(512)} %param.27) | copy-start | bytes 6148
  74.0 17.7 %copy-start.34 = (f32[512]{0:T(512)S(1)}, f32[512]{0:T(512)}, u32[]{:S(2)}) copy-start(f32[512]{0:T(512)} %param.26) | copy-start | bytes 6148
  101.7 4.4 copy-start.15
  101.7 4.4 copy-start.17
  101.7 4.4 copy-start.19
  101.7 4.4 copy-start.21
  103.1 2.0 copy-start.7
  106.2 3.9 copy-start.8
  109.2 0.8 copy-start.36
  134.7 157.8 %copy-start.32 = (f32[2048]{0:T(1024)S(1)}, f32[2048]{0:T(1024)}, u32[]{:S(2)}) copy-start(f32[2048]{0:T(1024)} %param.28) | copy-start | bytes 24580
  134.7 210.1 %all-gather.16.cloned.1.call-start = ((), (), s32[]{:S(2)}) async-start(), calls=%async_computation.12 | async-start | bytes 9437184 | tf_op jit(solution)/shard_map/all_gather | solution.py:133
  135.3 265.7 %all-gather.18.cloned.1.call-start = ((), (), s32[]{:S(2)}) async-start(), calls=%async_computation.13 | async-start | bytes 9437184 | tf_op jit(solution)/shard_map/all_gather | solution.py:134
  136.1 322.7 %all-gather.20.cloned.1.call-start = ((), (), s32[]{:S(2)}) async-start(), calls=%async_computation.14 | async-start | bytes 9437184 | tf_op jit(solution)/shard_map/all_gather | solution.py:135
  136.8 487.6 %all-reduce.10.cloned.1.call-start = ((), (), s32[]{:S(2)}) async-start(), calls=%async_computation.15 | async-start | bytes 8388608 | tf_op jit(solution)/shard_map/psum | solution.py:170
  289.8 3.4 copy-start
  469.3 157.9 %copy-start.33 = (f32[2048]{0:T(1024)S(1)}, f32[2048]{0:T(1024)}, u32[]{:S(2)}) copy-start(f32[2048]{0:T(1024)} %param.29) | copy-start | bytes 24580
  469.3 347.1 %all-reduce.12.cloned.1.call-start = ((), (), s32[]{:S(2)}) async-start(), calls=%async_computation.16 | async-start | bytes 8388608 | tf_op jit(solution)/shard_map/psum | solution.py:196
  624.4 3.4 copy-start.3
  644.9 7.8 copy-start.38
  662.3 294.9 %all-reduce.14.cloned.1.call-start = ((), (), s32[]{:S(2)}) async-start(), calls=%async_computation.17 | async-start | bytes 4194304 | tf_op jit(solution)/shard_map/psum | solution.py:234
  816.4 5.2 copy-start.1
  816.4 6.5 copy-start.4
  816.4 7.1 copy-start.5
  823.5 5.5 copy-start.26
  823.5 5.5 copy-start.30
  829.0 5.1 copy-start.10
  829.1 2.9 copy-start.9
  830.4 3.8 copy-start.37
  834.2 1.6 copy-start.20
  834.2 1.7 copy-start.22
  835.8 1.0 copy-start.16
  835.9 1.2 copy-start.18
  835.9 2.2 copy-start.23
  835.9 2.2 copy-start.24
  862.6 3.6 copy-start.27
  864.5 3.0 copy-start.13
  866.2 1.3 copy-start.11
  866.2 1.8 copy-start.28
  868.0 1.6 copy-start.25
  868.0 1.7 copy-start.29
  872.4 3.4 copy-start.14
  872.4 138.1 %reduce-scatter.12.cloned.1.call-start = ((), (), s32[]{:S(2)}) async-start(), calls=%async_computation.20 | async-start | bytes 4718592 | tf_op jit(solution)/shard_map/reduce_scatter | solution.py:241
  875.7 3.4 copy-start.12
  875.7 189.3 %reduce-scatter.8.cloned.1.call-start = ((), (), s32[]{:S(2)}) async-start(), calls=%async_computation.18 | async-start | bytes 4718592 | tf_op jit(solution)/shard_map/reduce_scatter | solution.py:239
  879.0 3.4 copy-start.31
  879.0 240.3 %reduce-scatter.10.cloned.1.call-start = ((), (), s32[]{:S(2)}) async-start(), calls=%async_computation.19 | async-start | bytes 4718592 | tf_op jit(solution)/shard_map/reduce_scatter | solution.py:240
  882.3 5.4 copy-start.6
  882.3 291.9 %reduce-scatter.14.cloned.1.call-start = ((), (), s32[]{:S(2)}) async-start(), calls=%async_computation.21 | async-start | bytes 4718592 | tf_op jit(solution)/shard_map/reduce_scatter | solution.py:242
  887.4 406.9 %reduce-scatter.20.cloned.1.call-start = ((), (), s32[]{:S(2)}) async-start(), calls=%async_computation.24 | async-start | bytes 18874368 | tf_op jit(solution)/shard_map/reduce_scatter | solution.py:245
  901.3 513.2 %reduce-scatter.18.cloned.1.call-start = ((), (), s32[]{:S(2)}) async-start(), calls=%async_computation.23 | async-start | bytes 18874368 | tf_op jit(solution)/shard_map/reduce_scatter | solution.py:244
  913.9 620.8 %reduce-scatter.16.cloned.1.call-start = ((), (), s32[]{:S(2)}) async-start(), calls=%async_computation.22 | async-start | bytes 18874368 | tf_op jit(solution)/shard_map/reduce_scatter | solution.py:243
Sparse Core Ops, SparseCore 0:
  9.9 30.4 all-gather.11
  42.3 27.7 all-gather.9
  72.0 27.7 all-gather.7
  101.5 28.0 all-gather.13
  134.8 154.9 all-reduce.7
  291.6 53.2 all-gather.15
  346.7 54.2 all-gather.17
  402.9 55.8 all-gather.19
  469.4 154.9 all-reduce.9
  662.4 153.9 all-reduce.11
  872.5 84.6 all-reduce.13
  960.4 50.0 reduce-scatter.11
  1013.9 51.0 reduce-scatter.7
  1068.2 51.0 reduce-scatter.9
  1123.1 51.0 reduce-scatter.13
  1178.2 115.9 reduce-scatter.19
  1298.3 116.1 reduce-scatter.17
  1418.5 116.1 reduce-scatter.15
where the time goes:
time: 1550 us; the launch traced here: 1540 us
  waiting for transfers between devices  1250 us (81%)
  matrix products  149 us (10%)
  other arithmetic  49.8 us (3%)
  blocking collectives  46.3 us (3%)
  local copies, waits for them, and re-layouts  32.1 us (2%)
  between operations  16 us (1%)
    psum x1, waiting for transfers between devices, on_device(): lax.psum(jnp.dot(act_bf, wd_full, preferred_element_type=jnp.float32), 'mp')  154 us
    psum x1, waiting for transfers between devices, on_device(): dh = dy + lax.psum(ffn_part, 'mp')  154 us
    psum x1, waiting for transfers between devices, on_device(): lax.psum(jnp.dot(o_flat, wo_full, preferred_element_type=jnp.float32), 'mp')  153 us
    reduce_scatter x1, waiting for transfers between devices, on_device(): lax.psum_scatter(g_gate, 'dp', scatter_dimension=0, tiled=True)  120 us
    reduce_scatter x1, waiting for transfers between devices, on_device(): lax.psum_scatter(g_up, 'dp', scatter_dimension=0, tiled=True)  120 us
    reduce_scatter x1, waiting for transfers between devices, on_device(): lax.psum_scatter(g_down, 'dp', scatter_dimension=1, tiled=True)  120 us
    reduce_scatter x1, waiting for transfers between devices, on_device(): lax.psum_scatter(g_output, 'dp', scatter_dimension=1, tiled=True)  52.9 us
    reduce_scatter x1, waiting for transfers between devices, on_device(): lax.psum_scatter(g_query, 'dp', scatter_dimension=0, tiled=True)  52.4 us
  transfers between devices with their start and end apart: 18, of which 17 were waited for; matrix products, arithmetic and copies ran while one was open for 8% of the time, Pallas kernels for 0%

commit v1 on v0

--- a/solution.py
+++ b/solution.py
@@ -7,6 +7,11 @@
 HD = 128
 EPS = 1e-06
 THETA = 500000.0
+
+
+def add_all(x, mesh_axis):
+    parts = lax.all_gather(x, mesh_axis)
+    return jnp.sum(parts, axis=0)
 
 
 def doc_positions(seg_row):
@@ -193,7 +198,7 @@
     ffn_part = jnp.dot(d_gate, wg_back.T, preferred_element_type=jnp.float32) + jnp.dot(
         d_up, wu_back.T, preferred_element_type=jnp.float32
     )
-    dh = dy + lax.psum(ffn_part, "mp")
+    dh = dy + add_all(ffn_part, "mp")
     g_down = jnp.dot(act_bf.T, d_ffn, preferred_element_type=jnp.float32)
     g_gate = jnp.dot(h_bf.T, d_gate, preferred_element_type=jnp.float32)
     g_up = jnp.dot(h_bf.T, d_up, preferred_element_type=jnp.float32)

time: 1550 us -> 1690 us (1.090)
  waiting for transfers between devices: 1250 us -> 1380 us
    all_gather x0 -> x1, waiting for transfers between devices: none -> 286 us  [add_all(): parts = lax.all_gather(x, mesh_axis)]
    psum x1 -> x0, waiting for transfers between devices: 154 us -> none  [on_device(): dh = dy + lax.psum(ffn_part, 'mp')]
where the time goes in v1:
time: 1690 us; the launch traced here: 1680 us
  waiting for transfers between devices  1380 us (82%)
  matrix products  150 us (9%)
  other arithmetic  60.1 us (4%)
  blocking collectives  45.2 us (3%)
  local copies, waits for them, and re-layouts  34.2 us (2%)
    all_gather x1, waiting for transfers between devices, add_all(): parts = lax.all_gather(x, mesh_axis)  286 us
    psum x1, waiting for transfers between devices, on_device(): lax.psum(jnp.dot(act_bf, wd_full, preferred_element_type=jnp.float32), 'mp')  154 us
    psum x1, waiting for transfers between devices, on_device(): lax.psum(jnp.dot(o_flat, wo_full, preferred_element_type=jnp.float32), 'mp')  153 us
    reduce_scatter x1, waiting for transfers between devices, on_device(): lax.psum_scatter(g_up, 'dp', scatter_dimension=0, tiled=True)  120 us
    reduce_scatter x1, waiting for transfers between devices, on_device(): lax.psum_scatter(g_gate, 'dp', scatter_dimension=0, tiled=True)  120 us
    reduce_scatter x1, waiting for transfers between devices, on_device(): lax.psum_scatter(g_down, 'dp', scatter_dimension=1, tiled=True)  118 us
    reduce_scatter x1, waiting for transfers between devices, on_device(): lax.psum_scatter(g_output, 'dp', scatter_dimension=1, tiled=True)  54.9 us
    reduce_scatter x1, waiting for transfers between devices, on_device(): lax.psum_scatter(g_query, 'dp', scatter_dimension=0, tiled=True)  52.4 us
  transfers between devices with their start and end apart: 18, of which 17 were waited for; matrix products, arithmetic and copies ran while one was open for 8% of the time, Pallas kernels for 0%

profile of v1, /device:TPU:0, one launch (start us, length us, event | category | flops | bytes accessed | tf_op | source)
XLA Modules:
  0.0 1684.0 jit_solution(10201621891980071070)
XLA Ops:
  12.5 1.8 multiply_cosine_fusion
  14.4 26.0 %all-gather.14.cloned.1.call-done = bf16[2048,512]{1,0:T(8,128)(2,1)} async-done(((bf16[256,512]{1,0:T(8,128)(2,1)}), bf16[2048,512]{1,0:T(8,128)(2,1)}) %all-gather.14.cloned.1.call-update) | async-done | bytes 2097168 | tf_op jit(solution)/shard_map/all_gather | solution.py:135
  40.4 3.5 multiply_reduce_fusion.9
  44.0 26.1 %all-gather.12.cloned.1.call-done = bf16[2048,512]{1,0:T(8,128)(2,1)} async-done(((bf16[256,512]{1,0:T(8,128)(2,1)}), bf16[2048,512]{1,0:T(8,128)(2,1)}) %all-gather.12.cloned.1.call-update) | async-done | bytes 2097168 | tf_op jit(solution)/shard_map/all_gather | solution.py:134
  70.1 3.9 multiply_reduce_fusion.10
  74.0 11.8 all-reduce.2
  87.0 2.4 copy.82
  89.4 2.4 copy.81
  94.1 2.4 copy.80
  96.5 2.4 copy.79
  98.8 2.9 subtract_convert_fusion.5
  103.2 2.0 copy-done.7
  106.2 3.0 convolution_convert_fusion.1
  110.0 2.2 convolution_convert_fusion.3
  112.2 17.5 %all-gather.16.cloned.1.call-done = bf16[512,2048]{1,0:T(8,128)(2,1)} async-done(((bf16[512,256]{1,0:T(8,128)(2,1)}), bf16[512,2048]{1,0:T(8,128)(2,1)}) %all-gather.16.cloned.1.call-update) | async-done | bytes 2097168 | tf_op jit(solution)/shard_map/all_gather | solution.py:137
  129.7 5.0 fusion.24
  137.1 152.8 %all-reduce.7.cloned.1.call-done = f32[512,2048]{1,0:T(8,128)} async-done(((f32[512,2048]{1,0:T(8,128)}), f32[512,2048]{1,0:T(8,128)}) %all-reduce.7.cloned.1.call-update) | async-done | bytes 4194320 | tf_op jit(solution)/shard_map/psum | solution.py:168
  289.9 2.7 multiply_reduce_fusion.5
  293.3 2.1 fusion.4
  295.4 49.5 %all-gather.18.cloned.1.call-done = bf16[2048,2048]{1,0:T(8,128)(2,1)} async-done(((bf16[256,2048]{1,0:T(8,128)(2,1)}), bf16[2048,2048]{1,0:T(8,128)(2,1)}) %all-gather.18.cloned.1.call-update) | async-done | bytes 8388624 | tf_op jit(solution)/shard_map/all_gather | solution.py:138
  344.9 10.6 fusion.25
  355.4 45.6 %all-gather.20.cloned.1.call-done = bf16[2048,2048]{1,0:T(8,128)(2,1)} async-done(((bf16[256,2048]{1,0:T(8,128)(2,1)}), bf16[2048,2048]{1,0:T(8,128)(2,1)}) %all-gather.20.cloned.1.call-update) | async-done | bytes 8388624 | tf_op jit(solution)/shard_map/all_gather | solution.py:139
  401.0 12.5 multiply_convert_fusion.4
  413.5 45.3 %all-gather.22.cloned.1.call-done = bf16[2048,2048]{1,0:T(8,128)(2,1)} async-done(((bf16[2048,256]{1,0:T(8,128)(2,1)}), bf16[2048,2048]{1,0:T(8,128)(2,1)}) %all-gather.22.cloned.1.call-update) | async-done | bytes 8388624 | tf_op jit(solution)/shard_map/all_gather | solution.py:140
  458.8 10.5 fusion.26
  470.4 154.0 %all-reduce.9.cloned.1.call-done = f32[512,2048]{1,0:T(8,128)} async-done(((f32[512,2048]{1,0:T(8,128)}), f32[512,2048]{1,0:T(8,128)}) %all-reduce.9.cloned.1.call-update) | async-done | bytes 4194320 | tf_op jit(solution)/shard_map/psum | solution.py:175
  624.4 2.7 multiply_reduce_fusion.4
  627.9 3.0 multiply_reduce_fusion
  630.8 14.1 multiply_convert_fusion.1
  645.0 7.8 fusion.27
  652.8 9.6 convolution_add_fusion
  662.4 285.8 %all-gather.24.cloned.1.call-done = f32[2048,2048]{1,0:T(8,128)} async-done(((f32[512,2048]{1,0:T(8,128)}), f32[2048,2048]{1,0:T(8,128)}) %all-gather.24.cloned.1.call-update) | async-done | bytes 16777232 | tf_op jit(solution)/shard_map/all_gather | solution.py:13
  948.2 10.2 reduce_sum.141
  958.4 5.2 multiply_reduce_fusion.1
  965.6 5.5 subtract_convert_fusion
  974.0 2.2 convolution_convert_fusion.2
  980.1 2.0 multiply_add_fusion.1
  983.5 2.6 copy.63
  987.6 2.9 pad_maximum_fusion
  990.5 2.5 copy.59
  993.0 1.9 fusion.10
  994.9 8.8 all-reduce.1
  1003.7 1.9 subtract_convert_fusion.3
  1010.8 2.7 add_convert_fusion
  1013.6 3.2 convolution_bitcast_fusion
  1016.9 3.2 convolution_bitcast_fusion.2
  1020.2 3.2 convolution_bitcast_fusion.1
  1025.0 13.5 fusion.20
  1038.6 12.6 fusion.32
  1051.5 12.9 fusion.31
  1065.5 4.8 fusion.30
  1070.4 24.6 %all-reduce = (f32[512]{0:T(512)}, f32[512]{0:T(512)}, f32[2048]{0:T(1024)}, f32[2048]{0:T(1024)}) all-reduce(f32[512]{0:T(512)S(1)} %get-tuple-element.45, f32[512]{0:T(512)S(1)} %get-tuple-element.43, f32[2048]{0:T(1024)S(1)} %get-tuple-element.39, f32[2048]{0:T(1024)S(1)} %get-tuple-element.41), channel_id=1, replica_groups=mesh['dp'=8,'mp'=4] {'dp'}, use_global_device_ids=true, to_apply=%region_29.30 | all-reduce | flops 5120 | bytes 40960 | tf_op jit(solution)/shard_map/psum | solution.py:252
  1095.0 4.2 all-reduce.11.cloned.1.call-done
  1099.1 6.1 convert_add_fusion
  1105.2 47.3 %reduce-scatter.12.cloned.1.call-done = f32[256,512]{0,1:T(8,128)} async-done(((f32[2048,512]{0,1:T(8,128)}), f32[256,512]{0,1:T(8,128)}) %reduce-scatter.12.cloned.1.call-update) | async-done | bytes 524304 | tf_op jit(solution)/shard_map/reduce_scatter | solution.py:246
  1152.5 2.0 copy.67
  1154.5 52.4 %reduce-scatter.8.cloned.1.call-done = f32[256,512]{0,1:T(8,128)} async-done(((f32[2048,512]{0,1:T(8,128)}), f32[256,512]{0,1:T(8,128)}) %reduce-scatter.8.cloned.1.call-update) | async-done | bytes 524304 | tf_op jit(solution)/shard_map/reduce_scatter | solution.py:244
  1206.9 2.0 copy.65
  1209.0 52.3 %reduce-scatter.10.cloned.1.call-done = f32[256,512]{0,1:T(8,128)} async-done(((f32[2048,512]{0,1:T(8,128)}), f32[256,512]{0,1:T(8,128)}) %reduce-scatter.10.cloned.1.call-update) | async-done | bytes 524304 | tf_op jit(solution)/shard_map/reduce_scatter | solution.py:245
  1261.3 2.0 copy.66
  1263.3 118.0 %reduce-scatter.20.cloned.1.call-done = f32[2048,256]{1,0:T(8,128)} async-done(((f32[2048,2048]{1,0:T(8,128)}), f32[2048,256]{1,0:T(8,128)}) %reduce-scatter.20.cloned.1.call-update) | async-done | bytes 2097168 | tf_op jit(solution)/shard_map/reduce_scatter | solution.py:250
  1381.3 120.2 %reduce-scatter.18.cloned.1.call-done = f32[256,2048]{1,0:T(8,128)} async-done(((f32[2048,2048]{1,0:T(8,128)}), f32[256,2048]{1,0:T(8,128)}) %reduce-scatter.18.cloned.1.call-update) | async-done | bytes 2097168 | tf_op jit(solution)/shard_map/reduce_scatter | solution.py:249
  1501.5 120.2 %reduce-scatter.16.cloned.1.call-done = f32[256,2048]{1,0:T(8,128)} async-done(((f32[2048,2048]{1,0:T(8,128)}), f32[256,2048]{1,0:T(8,128)}) %reduce-scatter.16.cloned.1.call-update) | async-done | bytes 2097168 | tf_op jit(solution)/shard_map/reduce_scatter | solution.py:248
  1621.7 54.9 %reduce-scatter.14.cloned.1.call-done = f32[512,256]{1,0:T(8,128)} async-done(((f32[512,2048]{1,0:T(8,128)}), f32[512,256]{1,0:T(8,128)}) %reduce-scatter.14.cloned.1.call-update) | async-done | bytes 524304 | tf_op jit(solution)/shard_map/reduce_scatter | solution.py:247
  (147 shorter events, 36.3 us)
Async XLA Ops:
  7.2 33.2 %all-gather.14.cloned.1.call-start = ((), (), s32[]{:S(2)}) async-start(), calls=%async_computation.9 | async-start | bytes 2359296 | tf_op jit(solution)/shard_map/all_gather | solution.py:135
  7.9 62.2 %all-gather.12.cloned.1.call-start = ((), (), s32[]{:S(2)}) async-start(), calls=%async_computation.8 | async-start | bytes 2359296 | tf_op jit(solution)/shard_map/all_gather | solution.py:134
  8.7 97.5 %all-gather.10.cloned.1.call-start = ((), (), s32[]{:S(2)}) async-start(), calls=%async_computation.7 | async-start | bytes 2359296 | tf_op jit(solution)/shard_map/all_gather | solution.py:136
  9.4 120.3 %all-gather.16.cloned.1.call-start = ((), (), s32[]{:S(2)}) async-start(), calls=%async_computation.10 | async-start | bytes 2359296 | tf_op jit(solution)/shard_map/all_gather | solution.py:137
  10.0 279.9 %all-reduce.7.cloned.1.call-start = ((), (), s32[]{:S(2)}) async-start(), calls=%async_computation.11 | async-start | bytes 8388608 | tf_op jit(solution)/shard_map/psum | solution.py:168
  14.4 55.7 %copy-start.3 = (bf16[512,2048]{1,0:T(8,128)(2,1)S(1)}, bf16[512,2048]{1,0:T(8,128)(2,1)}, u32[]{:S(2)}) copy-start(bf16[512,2048]{1,0:T(8,128)(2,1)} %param.15) | copy-start | bytes 6291460
  43.9 41.9 %copy-start.35 = (f32[512]{0:T(512)S(1)}, f32[512]{0:T(512)}, u32[]{:S(2)}) copy-start(f32[512]{0:T(512)} %param.27) | copy-start | bytes 6148
  74.0 17.7 %copy-start.34 = (f32[512]{0:T(512)S(1)}, f32[512]{0:T(512)}, u32[]{:S(2)}) copy-start(f32[512]{0:T(512)} %param.26) | copy-start | bytes 6148
  101.7 4.4 copy-start.15
  101.7 4.4 copy-start.17
  101.8 4.4 copy-start.19
  101.8 4.4 copy-start.21
  103.2 2.0 copy-start.7
  106.2 3.9 copy-start.8
  109.2 0.8 copy-start.36
  134.7 157.8 %copy-start.32 = (f32[2048]{0:T(1024)S(1)}, f32[2048]{0:T(1024)}, u32[]{:S(2)}) copy-start(f32[2048]{0:T(1024)} %param.28) | copy-start | bytes 24580
  134.7 210.1 %all-gather.18.cloned.1.call-start = ((), (), s32[]{:S(2)}) async-start(), calls=%async_computation.12 | async-start | bytes 9437184 | tf_op jit(solution)/shard_map/all_gather | solution.py:138
  135.3 265.7 %all-gather.20.cloned.1.call-start = ((), (), s32[]{:S(2)}) async-start(), calls=%async_computation.13 | async-start | bytes 9437184 | tf_op jit(solution)/shard_map/all_gather | solution.py:139
  136.1 322.7 %all-gather.22.cloned.1.call-start = ((), (), s32[]{:S(2)}) async-start(), calls=%async_computation.14 | async-start | bytes 9437184 | tf_op jit(solution)/shard_map/all_gather | solution.py:140
  136.8 487.6 %all-reduce.9.cloned.1.call-start = ((), (), s32[]{:S(2)}) async-start(), calls=%async_computation.15 | async-start | bytes 8388608 | tf_op jit(solution)/shard_map/psum | solution.py:175
  289.8 3.4 copy-start
  469.3 157.9 %copy-start.33 = (f32[2048]{0:T(1024)S(1)}, f32[2048]{0:T(1024)}, u32[]{:S(2)}) copy-start(f32[2048]{0:T(1024)} %param.29) | copy-start | bytes 24580
  469.3 478.9 %all-gather.24.cloned.1.call-start = ((), (), s32[]{:S(2)}) async-start(), calls=%async_computation.24 | async-start | bytes 20971520 | tf_op jit(solution)/shard_map/all_gather | solution.py:13
  624.4 3.4 copy-start.4
  645.0 7.8 copy-start.38
  662.3 436.8 %all-reduce.11.cloned.1.call-start = ((), (), s32[]{:S(2)}) async-start(), calls=%async_computation.16 | async-start | bytes 4194304 | tf_op jit(solution)/shard_map/psum | solution.py:239
  958.4 5.2 copy-start.1
  958.4 6.5 copy-start.2
  958.4 7.1 copy-start.5
  965.6 5.5 copy-start.26
  965.6 5.5 copy-start.30
  971.0 5.1 copy-start.10
  971.0 2.9 copy-start.9
  972.3 3.8 copy-start.37
  976.2 1.7 copy-start.20
  976.2 1.7 copy-start.22
  977.8 1.0 copy-start.16
  977.8 1.2 copy-start.18
  977.9 2.2 copy-start.23
  977.9 2.2 copy-start.24
  1003.7 3.6 copy-start.27
  1005.6 3.0 copy-start.13
  1007.3 1.3 copy-start.11
  1007.3 1.8 copy-start.28
  1009.1 1.6 copy-start.25
  1009.1 1.7 copy-start.29
  1013.5 3.4 copy-start.14
  1013.5 139.0 %reduce-scatter.12.cloned.1.call-start = ((), (), s32[]{:S(2)}) async-start(), calls=%async_computation.19 | async-start | bytes 4718592 | tf_op jit(solution)/shard_map/reduce_scatter | solution.py:246
  1016.8 3.4 copy-start.12
  1016.8 190.1 %reduce-scatter.8.cloned.1.call-start = ((), (), s32[]{:S(2)}) async-start(), calls=%async_computation.17 | async-start | bytes 4718592 | tf_op jit(solution)/shard_map/reduce_scatter | solution.py:244
  1020.1 241.1 %reduce-scatter.10.cloned.1.call-start = ((), (), s32[]{:S(2)}) async-start(), calls=%async_computation.18 | async-start | bytes 4718592 | tf_op jit(solution)/shard_map/reduce_scatter | solution.py:245
  1023.4 1.6 copy-start.6
  1023.4 357.9 %reduce-scatter.20.cloned.1.call-start = ((), (), s32[]{:S(2)}) async-start(), calls=%async_computation.23 | async-start | bytes 18874368 | tf_op jit(solution)/shard_map/reduce_scatter | solution.py:250
  1038.6 463.0 %reduce-scatter.18.cloned.1.call-start = ((), (), s32[]{:S(2)}) async-start(), calls=%async_computation.22 | async-start | bytes 18874368 | tf_op jit(solution)/shard_map/reduce_scatter | solution.py:249
  1051.2 570.5 %reduce-scatter.16.cloned.1.call-start = ((), (), s32[]{:S(2)}) async-start(), calls=%async_computation.21 | async-start | bytes 18874368 | tf_op jit(solution)/shard_map/reduce_scatter | solution.py:248
  1064.4 1.1 copy-start.31
  1064.5 612.1 %reduce-scatter.14.cloned.1.call-start = ((), (), s32[]{:S(2)}) async-start(), calls=%async_computation.20 | async-start | bytes 4718592 | tf_op jit(solution)/shard_map/reduce_scatter | solution.py:247
Sparse Core Ops, SparseCore 0:
  9.9 30.4 all-gather.13
  42.3 27.7 all-gather.11
  72.0 27.7 all-gather.9
  101.5 28.0 all-gather.15
  134.8 154.9 all-reduce.6
  291.6 53.2 all-gather.17
  346.7 54.2 all-gather.19
  402.9 55.8 all-gather.21
  469.4 154.9 all-reduce.8
  662.5 285.7 all-gather.23
  1013.6 85.4 all-reduce.10
  1102.3 50.0 reduce-scatter.11
  1155.8 51.0 reduce-scatter.7
  1210.2 51.0 reduce-scatter.9
  1265.3 115.9 reduce-scatter.19
  1385.3 116.2 reduce-scatter.17
  1505.5 116.1 reduce-scatter.15
  1625.5 51.0 reduce-scatter.13
